TPU v7x, 32 devices: a whole 2x2x4 slice. The times are simulated.
32 devices in a mesh: grp: 4 (over x, core), mem: 8 (over z, y).
Axes of the slice: x: 2, y: 2, z: 4, core: 2. Of those that a mesh axis runs over, the one named last changes fastest.
Arguments:
- images: bfloat16 [4, 2, 768, 16384], P('grp', None, None, 'mem'), may hold values from -6 to 6
- phantom: bfloat16 [4, 16384], P('grp', 'mem'), may hold values from -12 to 12
- inject_rows: int32 [4, 2, 64], P('grp'), may hold values from 0 to 767
- prior_blocks: int32 [4, 2, 768], P('grp'), may hold values from 0 to 127
- basis: bfloat16 [16384, 512], P('mem'), may hold values from -0.046875 to 0.046875
- refs: bfloat16 [512, 32768], P(None, 'mem'), may hold values from -24 to 24
Outputs:
- new_refs: float32 [512, 32768], P('grp', 'mem')
Inputs may be any that keep to these rules, and one draw needn't show every extreme that they name: `inject_rows`: row numbers within a batch; repeats may occur. `prior_blocks`: orientation block numbers; block b holds orientations b * 256 to (b + 1) * 256 - 1.
All inputs are finite; a program needn't handle non-finite values.
Results may differ from a plain program's by a relative error of at most 0.0051.
Values sent between devices are 32-bit elements; how exact they have to be, the bound alone decides.
A program may use at most 128 MiB of HBM per device.

v0:
```python
import jax
import jax.numpy as jnp
from jax import lax
from jax.sharding import PartitionSpec as P

OBLOCK = 256


PRIOR_INCREMENT = 3.0


def make_term(pairs):
    final_output = None
    for basis_coefficients, weights in pairs:
        product = lax.dot_general(
            basis_coefficients,
            weights,
            (((0,), (0,)), ((), ())),
            preferred_element_type=jnp.float32,
        )
        final_output = product
    return final_output


def shards(images, phantom, inject_rows, prior_blocks, basis, refs):
    particles = images.shape[2]
    batch_groups = images.shape[1]
    local_orientation = refs.shape[1]
    positions = jnp.arange(particles, dtype=jnp.int32)
    orient_start = lax.axis_index("mem") * local_orientation
    orient_block = (orient_start + jnp.arange(local_orientation, dtype=jnp.int32)) // OBLOCK
    phantom_partial = jnp.dot(phantom[0], basis, preferred_element_type=jnp.float32)
    share_rows = basis.shape[1] // lax.axis_size("grp")
    shares = jnp.zeros((share_rows, local_orientation), jnp.float32)
    masses = jnp.zeros((local_orientation,), jnp.float32)
    for batch_index in range(batch_groups):
        chosen = jnp.any(inject_rows[0, batch_index][:, None] == positions[None, :], axis=0).astype(
            jnp.float32
        )
        partial_output = jnp.dot(images[0, batch_index], basis, preferred_element_type=jnp.float32)
        summed_plain, phantom_coef = lax.psum((partial_output, phantom_partial), "mem")
        basis_coefficients = (summed_plain + chosen[:, None] * phantom_coef[None, :]).astype(
            jnp.bfloat16
        )
        match_score = (prior_blocks[0, batch_index][:, None] == orient_block[None, :]).astype(
            jnp.float32
        )
        score_rows = (
            jnp.dot(basis_coefficients, refs, preferred_element_type=jnp.float32)
            + PRIOR_INCREMENT * match_score
        )
        local_top = jnp.max(score_rows, axis=1)
        row_top = lax.pmax(local_top, "mem")
        powers = jnp.exp(score_rows - row_top[:, None])
        row_total = lax.psum(jnp.sum(powers, axis=1), "mem")
        weights = (powers / row_total[:, None]).astype(jnp.bfloat16)
        basis_coefficients, weights, local_mass = (
            basis_coefficients,
            weights,
            jnp.sum(weights.astype(jnp.float32), axis=0),
        )
        shares = shares + lax.psum_scatter(
            make_term(((basis_coefficients, weights),)), "grp", scatter_dimension=0, tiled=True
        )
        masses = masses + lax.psum(local_mass, "grp")
    grp_start = lax.axis_index("grp") * share_rows
    ref_slice = lax.dynamic_slice_in_dim(refs, grp_start, share_rows, 0).astype(jnp.float32)
    return (shares + ref_slice) / (masses[None, :] + 1.0)


def solution(mesh):
    placed = (
        P("grp", None, None, "mem"),
        P("grp", "mem"),
        P("grp", None, None),
        P("grp", None, None),
        P("mem", None),
        P(None, "mem"),
    )
    return jax.shard_map(
        shards, mesh=mesh, in_specs=placed, out_specs=P("grp", "mem"), check_vma=False
    )
```

profile of v0, /device:TPU:0, one launch (start us, length us, event | category | flops | bytes accessed | tf_op | source)
XLA Modules:
  0.0 314.2 jit_solution(121362327245889597)
XLA Ops:
  6.5 0.0 copy-start
  6.5 0.0 all-reduce.5.cloned.1.call-start
  6.5 1.6 copy-done
  8.1 0.0 copy-start.9
  8.1 5.0 %fusion.4 = f32[768,512]{1,0:T(8,128)} fusion(bf16[2048,512]{1,0:T(8,128)(2,1)S(1)} %copy-done, bf16[1,2,768,2048]{3,2,1,0:T(8,128)(2,1)} %param.6), kind=kOutput, calls=%fused_computation.13 | convolution fusion | flops 1610612736 | bytes 6815744 | tf_op jit(solution)/shard_map/dot_general | solution.py:40
  13.1 0.0 copy-done.9
  13.1 0.0 copy-start.8
  13.1 0.0 copy-start.6
  13.1 0.0 copy-start.7
  13.1 2.9 fusion.6
  16.0 0.0 all-reduce.5.cloned.1.call-update
  16.1 0.0 reduce-scatter.2.cloned.1.call-start
  16.1 0.0 copy-done.8
  16.1 0.1 fusion.10
  16.3 0.0 copy-done.6
  16.3 0.4 fusion.15
  16.7 24.3 %psum.53 = f32[512]{0:T(512)S(1)} all-reduce(f32[512]{0:T(512)S(1)} %bitcast.21), channel_id=1, replica_groups=mesh['grp'=4,'mem'=8] {'mem'}, use_global_device_ids=true, to_apply=%region_2.3 | all-reduce | flops 512 | bytes 4096 | tf_op jit(solution)/shard_map/psum | solution.py:41
  41.0 0.0 copy-done.7
  41.0 106.9 %all-reduce.5.cloned.1.call-done = (f32[768,512]{1,0:T(8,128)}, f32[768,512]{1,0:T(8,128)}) async-done(((f32[768,512]{1,0:T(8,128)}, f32[768,512]{1,0:T(8,128)}), (f32[768,512]{1,0:T(8,128)}, f32[768,512]{1,0:T(8,128)})) %all-reduce.5.cloned.1.call-update) | async-done | bytes 3145744 | tf_op jit(solution)/shard_map/psum | solution.py:41
  147.9 0.0 copy-start.3
  147.9 0.0 copy-start.5
  147.9 5.9 %fusion.18 = f32[768,4096]{1,0:T(8,128)S(1)} fusion(bf16[512,4096]{1,0:T(8,128)(2,1)} %param.11, f32[768,512]{1,0:T(8,128)} %get-tuple-element.13, f32[512]{0:T(512)S(1)} %psum.53, f32[768]{0:T(1024)S(1)} %convert_element_type.37), kind=kOutput, calls=%fused_computation.43 | convolution fusion | flops 3222405120 | bytes 18355200 | tf_op jit(solution)/shard_map/dot_general | solution.py:49
  153.9 0.0 copy-start.2
  153.9 0.0 copy-done.3
  153.9 0.0 copy-done.5
  153.9 8.7 %fusion.3 = (f32[768]{0:T(1024)S(1)}, f32[768]{0:T(1024)S(1)}, f32[768,4096]{1,0:T(8,128)}) fusion(s32[4096]{0:T(1024)S(1)} %add_select_fusion, s32[768]{0:T(1024)S(1)} %get-tuple-element.9, f32[768,4096]{1,0:T(8,128)S(1)} %fusion.18, s32[768]{0:T(1024)S(1)} %get-tuple-element.10, bf16[512,4096]{1,0:T(8,128)(2,1)S(1)} %copy-done.5, ...), kind=kOutput, calls=%fused_computation.11 | convolution fusion | flops 3247569408 | bytes 30966784 | tf_op jit(solution)/shard_map/dot_general | solution.py:49
  162.6 0.0 copy-done.2
  162.6 19.7 %all-reduce.2 = (f32[768]{0:T(1024)S(1)}, f32[768]{0:T(1024)S(1)}) all-reduce(f32[768]{0:T(1024)S(1)} %get-tuple-element.7, f32[768]{0:T(1024)S(1)} %get-tuple-element.8), channel_id=1, replica_groups=mesh['grp'=4,'mem'=8] {'mem'}, use_global_device_ids=true, to_apply=%region_11.12 | all-reduce | flops 1536 | bytes 12288 | tf_op jit(solution)/shard_map/pmax | solution.py:53
  182.2 11.0 %fusion.1 = (f32[768]{0:T(1024)S(1)}, f32[768]{0:T(1024)S(1)}) fusion(f32[768,4096]{1,0:T(8,128)} %get-tuple-element.25, f32[768]{0:T(1024)S(1)} %get-tuple-element.15, s32[4096]{0:T(1024)S(1)} %add_select_fusion, s32[768]{0:T(1024)S(1)} %get-tuple-element.9, f32[768]{0:T(1024)S(1)} %get-tuple-element.16, f32[768,4096]{1,0:T(8,128)} %copy-done.2, ...), kind=kLoop, calls=%fused_computation.9 | loop fusion | flops 31455744 | bytes 25200640 | tf_op jit(solution)/shard_map/reduce_sum | solution.py:55
  193.3 17.6 %all-reduce = (f32[768]{0:T(1024)S(1)}, f32[768]{0:T(1024)S(1)}) all-reduce(f32[768]{0:T(1024)S(1)} %get-tuple-element.6, f32[768]{0:T(1024)S(1)} %get-tuple-element.5), channel_id=1, replica_groups=mesh['grp'=4,'mem'=8] {'mem'}, use_global_device_ids=true, to_apply=%region_6.7 | all-reduce | flops 1536 | bytes 12288 | tf_op jit(solution)/shard_map/psum | solution.py:55
  210.9 0.0 copy-start.4
  210.9 12.7 %convert_reduce_fusion = (f32[4096]{0:T(1024)S(1)}, bf16[768,4096]{1,0:T(8,128)(2,1)S(1)}, f32[4096]{0:T(1024)S(1)}, bf16[768,4096]{1,0:T(8,128)(2,1)S(1)}) fusion(f32[768]{0:T(1024)S(1)} %get-tuple-element.12, f32[768]{0:T(1024)S(1)} %get-tuple-element.15, f32[768,4096]{1,0:T(8,128)} %get-tuple-element.25, s32[4096]{0:T(1024)S(1)} %add_select_fusion, ...), kind=kLoop, calls=%fused_computation | loop fusion | flops 50323456 | bytes 37816320 | tf_op jit(solution)/shard_map/reduce_sum | solution.py:60
  223.6 0.0 copy-done.4
  223.6 3.7 %fusion.17 = f32[512,4096]{1,0:T(8,128)S(1)} fusion(bf16[768,4096]{1,0:T(8,128)(2,1)S(1)} %get-tuple-element.22, f32[768,512]{1,0:T(8,128)S(1)} %copy-done.4, f32[512]{0:T(512)S(1)} %psum.53, f32[768]{0:T(1024)S(1)} %convert_element_type.37), kind=kOutput, calls=%fused_computation.42 | convolution fusion | flops 3222405120 | bytes 16258048 | tf_op jit(solution)/shard_map/dot_general | solution.py:15
  227.3 6.4 %convolution_add_fusion = f32[512,4096]{1,0:T(8,128)} fusion(f32[512,4096]{1,0:T(8,128)S(1)} %fusion.17, bf16[768,4096]{1,0:T(8,128)(2,1)S(1)} %get-tuple-element.18, f32[768,512]{1,0:T(8,128)S(1)} %copy-done.3, f32[768]{0:T(1024)S(1)} %convert_element_type.40, f32[512]{0:T(512)S(1)} %psum.53), kind=kOutput, calls=%fused_computation.12 | convolution fusion | flops 3224502272 | bytes 24646656 | tf_op jit(solution)/shard_map/dot_general | solution.py:15
  233.7 0.0 copy-start.1
  233.7 0.0 reduce-scatter.2.cloned.1.call-update
  233.8 10.2 %psum.59 = f32[4096]{0:T(1024)S(1)} all-reduce(f32[4096]{0:T(1024)S(1)} %add.74), channel_id=1, replica_groups=mesh['grp'=4,'mem'=8] {'grp'}, use_global_device_ids=true, to_apply=%region_16.17 | all-reduce | flops 4096 | bytes 32768 | tf_op jit(solution)/shard_map/psum | solution.py:65
  244.0 59.9 %reduce-scatter.2.cloned.1.call-done = f32[128,4096]{1,0:T(8,128)} async-done(((f32[512,4096]{1,0:T(8,128)}), f32[128,4096]{1,0:T(8,128)}) %reduce-scatter.2.cloned.1.call-update) | async-done | bytes 2097168 | tf_op jit(solution)/shard_map/reduce_scatter | solution.py:62
  303.9 3.5 %add_divide_fusion = f32[128,4096]{1,0:T(8,128)} fusion(f32[128,4096]{1,0:T(8,128)} %reduce-scatter.2.cloned.1.call-done, f32[4096]{0:T(1024)S(1)} %broadcast_add_fusion, bf16[512,4096]{1,0:T(8,128)(2,1)} %param.11, s32[]{:T(128)S(6)} %select_n.13), kind=kLoop, calls=%fused_computation.19 | loop fusion | flops 1572864 | bytes 5259268 | tf_op jit(solution)/shard_map/div | solution.py:68
  307.4 0.0 copy-done.1
  (7 shorter events, 0.1 us)
Async XLA Ops:
  6.5 1.6 copy-start
  6.5 141.4 %all-reduce.5.cloned.1.call-start = ((), (), s32[]{:S(2)}) async-start(), calls=%async_computation.2 | async-start | bytes 6291456 | tf_op jit(solution)/shard_map/psum | solution.py:41
  8.1 5.0 %copy-start.9 = (bf16[1,2,768,2048]{3,2,1,0:T(8,128)(2,1)S(1)}, bf16[1,2,768,2048]{3,2,1,0:T(8,128)(2,1)}, u32[]{:S(2)}) copy-start(bf16[1,2,768,2048]{3,2,1,0:T(8,128)(2,1)} %param.6) | copy-start | bytes 18874372
  13.1 3.0 copy-start.8
  13.1 3.2 %copy-start.6 = (bf16[1,2048]{1,0:T(2,128)(2,1)S(1)}, bf16[1,2048]{1,0:T(2,128)(2,1)}, u32[]{:S(2)}) copy-start(bf16[1,2048]{1,0:T(2,128)(2,1)} %param.7) | copy-start | bytes 12292
  13.1 27.9 %copy-start.7 = (s32[1,2,768]{2,1,0:T(2,128)S(1)}, s32[1,2,768]{2,1,0:T(2,128)}, u32[]{:S(2)}) copy-start(s32[1,2,768]{2,1,0:T(2,128)} %param.9) | copy-start | bytes 18436
  16.1 287.9 %reduce-scatter.2.cloned.1.call-start = ((), (), s32[]{:S(2)}) async-start(), calls=%async_computation.1 | async-start | bytes 10485760 | tf_op jit(solution)/shard_map/reduce_scatter | solution.py:62
  147.9 5.9 %copy-start.3 = (f32[768,512]{1,0:T(8,128)S(1)}, f32[768,512]{1,0:T(8,128)}, u32[]{:S(2)}) copy-start(f32[768,512]{1,0:T(8,128)} %get-tuple-element.14) | copy-start | bytes 4718596
  147.9 6.0 %copy-start.5 = (bf16[512,4096]{1,0:T(8,128)(2,1)S(1)}, bf16[512,4096]{1,0:T(8,128)(2,1)}, u32[]{:S(2)}) copy-start(bf16[512,4096]{1,0:T(8,128)(2,1)} %param.11) | copy-start | bytes 12582916
  153.9 8.7 %copy-start.2 = (f32[768,4096]{1,0:T(8,128)}, f32[768,4096]{1,0:T(8,128)S(1)}, u32[]{:S(2)}) copy-start(f32[768,4096]{1,0:T(8,128)S(1)} %fusion.18) | copy-start | bytes 37748740
  210.9 12.7 %copy-start.4 = (f32[768,512]{1,0:T(8,128)S(1)}, f32[768,512]{1,0:T(8,128)}, u32[]{:S(2)}) copy-start(f32[768,512]{1,0:T(8,128)} %get-tuple-element.13) | copy-start | bytes 4718596
  233.7 73.7 %copy-start.1 = (bf16[2048,512]{1,0:T(8,128)(2,1)S(1)}, bf16[2048,512]{1,0:T(8,128)(2,1)}, u32[]{:S(2)}) copy-start(bf16[2048,512]{1,0:T(8,128)(2,1)} %param.10) | copy-start | bytes 6291460
Sparse Core Ops, SparseCore 0:
  16.2 131.7 all-reduce.4
  233.9 69.9 reduce-scatter.1
where the time goes:
time: 314 us
  waiting for transfers between devices  167 us (53%)
  blocking collectives  71.9 us (23%)
  matrix products  33 us (11%)
  other arithmetic  27.3 us (9%)
  between operations  13.6 us (4%)
    psum x1, waiting for transfers between devices, shards(): lax.psum((partial_output, phantom_partial), 'mem')  107 us
    reduce_scatter x1, waiting for transfers between devices, shards(): lax.psum_scatter(make_term(((basis_coefficients, weights),)), 'grp', scat...  59.9 us
    psum x1, blocking collectives, shards(): lax.psum((partial_output, phantom_partial), 'mem')  24.3 us
    pmax x1, blocking collectives, shards(): row_top = lax.pmax(local_top, 'mem')  19.7 us
    psum x1, blocking collectives, shards(): row_total = lax.psum(jnp.sum(powers, axis=1), 'mem')  17.6 us
    dot_general x2, matrix products, shards(): jnp.dot(basis_coefficients, refs, preferred_element_type=jnp.float32)  14.6 us
    reduce_sum x1, other arithmetic, shards(): jnp.sum(weights.astype(jnp.float32), axis=0)  12.7 us
    reduce_sum x1, other arithmetic, shards(): row_total = lax.psum(jnp.sum(powers, axis=1), 'mem')  11 us
  transfers between devices with their start and end apart: 2, of which 2 were waited for; matrix products, arithmetic and copies ran while one was open for 0% of the time, Pallas kernels for 0%

commit v1 on v0

v1 whole, which is shorter than its diff:
```python
import functools

import jax
import jax.numpy as jnp
from jax import lax
from jax.experimental import pallas as pl
from jax.experimental.pallas import tpu as pltpu
from jax.sharding import PartitionSpec as P

OBLOCK = 256
PRIOR_INCREMENT = 3.0
MESH = pl.DeviceIdType.MESH
F32 = jnp.float32


def remote(src, dst, send_sem, recv_sem, device):
    return pltpu.make_async_remote_copy(
        src_ref=src, dst_ref=dst, send_sem=send_sem, recv_sem=recv_sem,
        device_id=device, device_id_type=MESH,
    )


def coeff_kernel(
    A, R, H,
    img, pha, chosen, basis, out,
    part0, part1, y0r, z0s, z0r, z1r, y1s, y1r, g0, g1,
    y0_ss, y0_rs, z0_ss, z0_rs, z1_ss, z1_rs, y1_ss, y1_rs,
    gz0_ss, gz0_rs, gy0_ss, gy0_rs, gy1_ss, gy1_rs, gz1_ss, gz1_rs,
):
    grp = lax.axis_index("grp")
    mem = lax.axis_index("mem")
    a, b = mem // 2, lax.rem(mem, 2)
    nb = 1 - b
    HR = R // 2
    ypeer = (grp, a * 2 + nb)

    def zpeer(k):
        return (grp, lax.rem(a + k, A) * 2 + b)

    barrier = pltpu.get_barrier_semaphore()
    pl.semaphore_signal(barrier, inc=1, device_id=ypeer, device_id_type=MESH)
    for k in range(1, A):
        pl.semaphore_signal(barrier, inc=1, device_id=zpeer(k), device_id_type=MESH)
    pl.semaphore_wait(barrier, A)

    phc = jnp.dot(pha[...], basis[...], preferred_element_type=F32)[0:1]

    def partial(k, bb, half):
        start = pl.multiple_of((lax.rem(a + k, A) * 2 + bb) * R, R)
        cols = slice(half * H, (half + 1) * H)
        plain = jnp.dot(img[pl.ds(start, R), :], basis[:, cols], preferred_element_type=F32)
        return plain + chosen[pl.ds(start, R), :] * phc[:, cols]

    ring = A == 4
    far = {0: 1, 1: A - 1}

    def zlink(k, h):
        return zpeer(far[h]) if ring and k == 2 else zpeer(k)

    near = [1, 3] if ring else list(range(1, A))
    pairs = [(k, h) for k in range(1, A) for h in range(2)]
    late = [(1, 0), (3, 1)] if ring else []
    y0 = [remote(part0.at[1, k], y0r.at[k], y0_ss.at[k], y0_rs.at[k], ypeer) for k in range(A)]
    z1 = {
        (k, h): remote(part1.at[k, h], z1r.at[k - 1, h], z1_ss.at[k - 1, h], z1_rs.at[k - 1, h], zlink(k, h))
        for k, h in pairs
    }
    order = [2, 1, 3, 0] if ring else [k % A for k in range(1, A + 1)]
    for k in order:
        part0[1, k] = partial(k, nb, 0)
        if k > 0:
            part1[k, 0] = partial(k, b, 1)
            part1[k, 1] = partial(k, nb, 1)
        y0[k].start()
        for h in range(2):
            if k > 0 and (k, h) not in late:
                z1[k, h].start()
    for k in order:
        part0[0, k] = partial(k, b, 0)
    part1[0, 0] = partial(0, b, 1)
    part1[0, 1] = partial(0, nb, 1)

    z0 = {
        (k, h): remote(z0s.at[k - 1, h], z0r.at[k - 1, h], z0_ss.at[k - 1, h], z0_rs.at[k - 1, h], zlink(k, h))
        for k, h in pairs
    }
    for k, h in late:
        z1[2, h].wait_recv()
        part1[k, h] = part1[k, h] + z1r[1, h]
        z1[k, h].start()
    for k in order[:-1]:
        y0[k].wait_recv()
        value = part0[0, k] + y0r[k]
        for h in range(2):
            z0s[k - 1, h] = value[h * HR:(h + 1) * HR]
            if (k, h) not in late:
                z0[k, h].start()
    for k, h in late:
        z0[2, h].wait_recv()
        z0s[k - 1, h] = z0s[k - 1, h] + z0r[1, h]
        z0[k, h].start()
    peer_sum = part1[0, 1]
    own_sum = part1[0, 0]
    for k in near:
        z1[k, 1].wait_recv()
        peer_sum = peer_sum + z1r[k - 1, 1]
    y1s[...] = peer_sum
    y1 = remote(y1s, y1r, y1_ss, y1_rs, ypeer)
    y1.start()
    for k in near:
        z1[k, 0].wait_recv()
        own_sum = own_sum + z1r[k - 1, 0]

    y0[0].wait_recv()
    mine0 = part0[0, 0] + y0r[0]
    for h in range(2):
        value = mine0[h * HR:(h + 1) * HR]
        for k in near:
            z0[k, h].wait_recv()
            value = value + z0r[k - 1, h]
        g0[0, 0, h] = value.astype(jnp.bfloat16).astype(F32)
    gz0 = {}
    gz1 = {}
    for k, h in pairs:
        source = far[h] if ring and k == 2 else 0
        gz0[k, h] = remote(
            g0.at[0, source, h], g0.at[0, k, h], gz0_ss.at[k - 1, h], gz0_rs.at[k - 1, h], zlink(k, h)
        )
        gz1[k, h] = remote(
            g1.at[source, h], g1.at[k, h], gz1_ss.at[k - 1, h], gz1_rs.at[k - 1, h], zlink(k, h)
        )
    gy0 = [remote(g0.at[0, k], g0.at[1, k], gy0_ss.at[k], gy0_rs.at[k], ypeer) for k in range(A)]
    for k, h in late + [(k, h) for k in near for h in range(2) if (k, h) not in late]:
        gz0[k, h].start()
    gy0[0].start()
    y1.wait_recv()
    g1[0, 0] = (own_sum + y1r[...]).astype(jnp.bfloat16).astype(F32)
    gy1 = remote(g1.at[0, 0], g1.at[0, 1], gy1_ss, gy1_rs, ypeer)
    gy1.start()
    for k in near:
        gz1[k, 0].start()
    for k, h in late:
        gz0[k, h].wait_recv()
        gz0[2, h].start()
    gy1.wait_recv()
    for k in near[::-1]:
        gz1[k, 1].start()
    for k in near:
        for h in range(2):
            if (k, h) not in late:
                gz0[k, h].wait_recv()
        gy0[k].start()
    for k, h in late:
        gz1[k, h].wait_recv()
        gz1[2, h].start()
    if ring:
        for h in range(2):
            gz0[2, h].wait_recv()
        gy0[2].start()

    def put(k, bb, half, value):
        start = pl.multiple_of((lax.rem(a - k + A, A) * 2 + bb) * R, R)
        out[pl.ds(start, R), half * H:(half + 1) * H] = value.astype(jnp.bfloat16)

    def both(e, k):
        return jnp.concatenate([g0[e, k, 0], g0[e, k, 1]], axis=0)

    put(0, b, 0, both(0, 0))
    put(0, b, 1, g1[0, 0])
    put(0, nb, 1, g1[0, 1])
    for k in range(1, A):
        put(k, b, 0, both(0, k))
    for k in near + ([2] if ring else []):
        for h in range(2):
            if (k, h) not in late:
                gz1[k, h].wait_recv()
        put(k, b, 1, g1[k, 0])
        put(k, nb, 1, g1[k, 1])
    for k in range(A):
        gy0[k].wait_recv()
        put(k, nb, 0, both(1, k))
    for k in range(A):
        y0[k].wait_send()
        gy0[k].wait_send()
    for pair in pairs:
        z0[pair].wait_send()
        z1[pair].wait_send()
        gz0[pair].wait_send()
        gz1[pair].wait_send()
    y1.wait_send()
    gy1.wait_send()


def coefficients(n_mem, img, pha, chosen, basis):
    rows, pixels = img.shape
    eigen = basis.shape[1]
    A, R, H = n_mem // 2, rows // n_mem, eigen // 2
    V = lambda *s: pltpu.VMEM(s, F32)
    D = lambda *s: pltpu.SemaphoreType.DMA(s)
    return pl.pallas_call(
        functools.partial(coeff_kernel, A, R, H),
        out_shape=jax.ShapeDtypeStruct((rows, eigen), jnp.bfloat16),
        in_specs=[pl.BlockSpec(memory_space=pltpu.VMEM)] * 4,
        out_specs=pl.BlockSpec(memory_space=pltpu.VMEM),
        scratch_shapes=[
            V(2, A, R, H), V(A, 2, R, H), V(A, R, H), V(A - 1, 2, R // 2, H), V(A - 1, 2, R // 2, H),
            V(A - 1, 2, R, H),
            V(R, H), V(R, H), V(2, A, 2, R // 2, H), V(A, 2, R, H),
            D(A), D(A), D(A - 1, 2), D(A - 1, 2), D(A - 1, 2), D(A - 1, 2),
            pltpu.SemaphoreType.DMA, pltpu.SemaphoreType.DMA,
            D(A - 1, 2), D(A - 1, 2), D(A), D(A),
            pltpu.SemaphoreType.DMA, pltpu.SemaphoreType.DMA, D(A - 1, 2), D(A - 1, 2),
        ],
        compiler_params=pltpu.CompilerParams(
            collective_id=0, has_side_effects=True, vmem_limit_bytes=48 * 1024 * 1024
        ),
    )(img, pha, chosen, basis)


def turn_to_row(col):
    return jnp.broadcast_to(col, (128, 128)).T[0:1]


def turn_to_col(row):
    return jnp.broadcast_to(row, (128, 128)).T[:, 0:1]


def update_kernel(
    M, X, NC, CW, RB, TR,
    coef, coef_t, prior, refs, out,
    p, stat, stat_r, scale, tot, mass, cr, cmr, xs, xms, xr, xmr,
    st_ss, st_rs, c_ss, c_rs, cm_ss, cm_rs, x_ss, x_rs, xm_ss, xm_rs,
):
    grp = lax.axis_index("grp")
    mem = lax.axis_index("mem")
    x, c = grp // 2, lax.rem(grp, 2)
    nc = 1 - c
    core = (x * 2 + nc, mem)
    rows = coef.shape[0]
    orient = refs.shape[1]
    S = rows // 128

    def xpeer(k):
        return (lax.rem(x + k, X) * 2 + c, mem)

    def mpeer(k):
        return (grp, lax.rem(mem + k, M))

    barrier = pltpu.get_barrier_semaphore()
    pl.semaphore_signal(barrier, inc=1, device_id=core, device_id_type=MESH)
    for k in range(1, X):
        pl.semaphore_signal(barrier, inc=1, device_id=xpeer(k), device_id_type=MESH)
    for k in range(1, M):
        pl.semaphore_signal(barrier, inc=1, device_id=mpeer(k), device_id_type=MESH)
    pl.semaphore_wait(barrier, X + M - 1)

    first_block = mem * (orient // OBLOCK)

    def score(t, carry):
        at = pl.ds(pl.multiple_of(t * TR, TR), TR)
        cf = coef[at, :]
        pr = prior[at, :]
        top = None
        for j in range(NC):
            s = jnp.dot(cf, refs[:, j * CW:(j + 1) * CW], preferred_element_type=F32)
            for i in range(CW // OBLOCK):
                inc = jnp.where(pr == first_block + (j * (CW // OBLOCK) + i), PRIOR_INCREMENT, 0.0).astype(F32)
                piece = s[:, i * OBLOCK:(i + 1) * OBLOCK] + inc
                p[at, j * CW + i * OBLOCK:j * CW + (i + 1) * OBLOCK] = piece
                high = jnp.max(piece, axis=1, keepdims=True)
                top = high if top is None else jnp.maximum(top, high)
        total = jnp.zeros((TR, 1), F32)
        for j in range(orient // OBLOCK):
            cols = slice(j * OBLOCK, (j + 1) * OBLOCK)
            e = jnp.exp(p[at, cols] - top)
            p[at, cols] = e
            total = total + jnp.sum(e, axis=1, keepdims=True)
        for i in range(TR // 128):
            stat[pl.ds(t * (TR // 128) + i, 1), :] = turn_to_row(top[i * 128:(i + 1) * 128])
            stat[pl.ds(S + t * (TR // 128) + i, 1), :] = turn_to_row(total[i * 128:(i + 1) * 128])
        return carry

    lax.fori_loop(0, rows // TR, score, 0)

    st = [None] + [
        remote(stat, stat_r.at[k - 1], st_ss.at[k - 1], st_rs.at[k - 1], mpeer(k)) for k in range(1, M)
    ]
    for k in range(1, M):
        st[k].start()
    for k in range(1, M):
        st[k].wait_recv()
    mine = stat[0:S, :]
    high = mine
    for k in range(1, M):
        high = jnp.maximum(high, stat_r[k - 1, 0:S, :])
    total = stat[S:2 * S, :] * jnp.exp(mine - high)
    for k in range(1, M):
        total = total + stat_r[k - 1, S:2 * S, :] * jnp.exp(stat_r[k - 1, 0:S, :] - high)
    factor = jnp.exp(mine - high) / total
    for i in range(S):
        scale[i * 128:(i + 1) * 128, :] = turn_to_col(factor[i:i + 1])

    def block_rows(k, cc):
        return pl.ds(pl.multiple_of((lax.rem(x + k, X) * 2 + cc) * RB, RB), RB)

    def c_copy(j, k):
        return remote(tot.at[j, block_rows(k, nc), :], cr.at[j, k], c_ss.at[j, k], c_rs.at[j, k], core)

    def cm_copy(j):
        return remote(mass.at[j], cmr.at[j], cm_ss.at[j], cm_rs.at[j], core)

    def x_copy(j, k):
        return remote(xs.at[j, k - 1], xr.at[j, k - 1], x_ss.at[j, k - 1], x_rs.at[j, k - 1], xpeer(k))

    def xm_copy(j, k):
        return remote(xms.at[j], xmr.at[j, k - 1], xm_ss.at[j, k - 1], xm_rs.at[j, k - 1], xpeer(k))

    def step(j, carry):
        @pl.when(j < NC)
        def _():
            cols = pl.ds(pl.multiple_of(j * CW, CW), CW)
            w = (p[:, cols] * scale[...]).astype(jnp.bfloat16)
            tot[j] = jnp.dot(coef_t[...], w, preferred_element_type=F32)
            mass[j] = jnp.broadcast_to(jnp.sum(w.astype(F32), axis=0, keepdims=True), (8, CW))
            for k in range(1, X):
                c_copy(j, k).start()
            cm_copy(j).start()
            c_copy(j, 0).start()

        @pl.when(j >= 1)
        def _():
            i = j - 1
            for k in range(1, X):
                c_copy(i, k).wait_recv()
                xs[i, k - 1] = tot[i, block_rows(k, c), :] + cr[i, k]
                x_copy(i, k).start()
            cm_copy(i).wait_recv()
            xms[i] = mass[i] + cmr[i]
            for k in range(1, X):
                xm_copy(i, k).start()

        return carry

    lax.fori_loop(0, NC + 1, step, 0)

    own_rows = block_rows(0, c)

    def finish(j, carry):
        cols = pl.ds(pl.multiple_of(j * CW, CW), CW)
        c_copy(j, 0).wait_recv()
        value = tot[j, own_rows, :] + cr[j, 0]
        m = xms[j]
        for k in range(1, X):
            x_copy(j, k).wait_recv()
            xm_copy(j, k).wait_recv()
            value = value + xr[j, k - 1]
            m = m + xmr[j, k - 1]
        out[:, cols] = (value + refs[own_rows, cols].astype(F32)) / (m[0:1] + 1.0)
        for k in range(X):
            c_copy(j, k).wait_send()
        cm_copy(j).wait_send()
        for k in range(1, X):
            x_copy(j, k).wait_send()
            xm_copy(j, k).wait_send()
        return carry

    lax.fori_loop(0, NC, finish, 0)
    for k in range(1, M):
        st[k].wait_send()


def update(n_grp, n_mem, coef, coef_t, prior, refs):
    rows, eigen = coef.shape
    orient = refs.shape[1]
    CW = min(512, orient)
    NC, RB, X, M = orient // CW, eigen // n_grp, n_grp // 2, n_mem
    S = rows // 128
    V = lambda *s: pltpu.VMEM(s, F32)
    D = lambda *s: pltpu.SemaphoreType.DMA(s)
    return pl.pallas_call(
        functools.partial(update_kernel, M, X, NC, CW, RB, 256),
        out_shape=jax.ShapeDtypeStruct((RB, orient), F32),
        in_specs=[pl.BlockSpec(memory_space=pltpu.VMEM)] * 4,
        out_specs=pl.BlockSpec(memory_space=pltpu.VMEM),
        scratch_shapes=[
            V(rows, orient), V(2 * S, 128), V(M - 1, 2 * S, 128), V(rows, 1),
            V(NC, eigen, CW), V(NC, 8, CW), V(NC, X, RB, CW), V(NC, 8, CW),
            V(NC, X - 1, RB, CW), V(NC, 8, CW), V(NC, X - 1, RB, CW), V(NC, X - 1, 8, CW),
            D(M - 1), D(M - 1), D(NC, X), D(NC, X), D(NC), D(NC),
            D(NC, X - 1), D(NC, X - 1), D(NC, X - 1), D(NC, X - 1),
        ],
        compiler_params=pltpu.CompilerParams(
            collective_id=1, has_side_effects=True, vmem_limit_bytes=67043328
        ),
    )(coef, coef_t, prior, refs)


def shards(n_grp, n_mem, images, phantom, inject_rows, prior_blocks, basis, refs):
    batches, particles, pixels = images.shape[1:]
    positions = jnp.arange(particles, dtype=jnp.int32)
    chosen = jnp.any(inject_rows[0][:, :, None] == positions[None, None, :], axis=1)
    chosen = chosen.astype(F32).reshape(batches * particles, 1)
    img = images.reshape(batches * particles, pixels)
    pha = jnp.broadcast_to(phantom, (16, pixels))
    coef = coefficients(n_mem, img, pha, chosen, basis)
    return update(n_grp, n_mem, coef, coef.T, prior_blocks.reshape(batches * particles, 1), refs)


def solution(mesh):
    placed = (
        P("grp", None, None, "mem"),
        P("grp", "mem"),
        P("grp", None, None),
        P("grp", None, None),
        P("mem", None),
        P(None, "mem"),
    )
    return jax.shard_map(
        functools.partial(shards, mesh.shape["grp"], mesh.shape["mem"]),
        mesh=mesh, in_specs=placed, out_specs=P("grp", "mem"), check_vma=False,
    )
```

time: 314 us -> 180 us (0.57)
  Pallas kernels: 0 us -> 168 us
  waiting for transfers between devices: 167 us -> 0 us
  blocking collectives: 71.9 us -> 0 us
  matrix products: 33 us -> 0 us
  other arithmetic: 27.3 us -> 1.54 us
  between operations: 13.6 us -> 0.07 us
  local copies, waits for them, and re-layouts: 1.65 us -> 9.59 us
    pallas_call x0 -> x2, Pallas kernels: none -> 168 us  [the longest x1 87.7 us: coefficients(): pl.pallas_call(functools.partial(coeff_kernel, A, R, H), out_shape=jax.Sh...]
    psum x1 -> x0, waiting for transfers between devices: 107 us -> none  [shards(): lax.psum((partial_output, phantom_partial), 'mem')]
    reduce_scatter x1 -> x0, waiting for transfers between devices: 59.9 us -> none  [shards(): lax.psum_scatter(make_term(((basis_coefficients, weights),)), 'grp', scat...]
    psum x3 -> x0, blocking collectives: 52.2 us -> none  [the longest x1 24.3 us: shards(): lax.psum((partial_output, phantom_partial), 'mem')]
    dot_general x7 -> x0, matrix products: 33 us -> none  [the longest x2 14.6 us: shards(): jnp.dot(basis_coefficients, refs, preferred_element_type=jnp.float32)]
    reduce_sum x2 -> x0, other arithmetic: 23.7 us -> none  [the longest x1 12.7 us: shards(): jnp.sum(weights.astype(jnp.float32), axis=0)]
    pmax x1 -> x0, blocking collectives: 19.7 us -> none  [shards(): row_top = lax.pmax(local_top, 'mem')]
    unnamed x20 -> x9, local copies, waits for them, and re-layouts: 1.62 us -> 8.03 us
  transfers between devices with their start and end apart: 2 -> 0, of which waited for: 2 -> 0; matrix products, arithmetic and copies ran while one was open for 0% -> 0% of each run, Pallas kernels for 0% -> 0%
where the time goes in v1:
time: 180 us; the launch traced here: 179 us
  Pallas kernels  168 us (93%)
  local copies, waits for them, and re-layouts  9.59 us (5%)
    pallas_call x1, Pallas kernels, coefficients(): pl.pallas_call(functools.partial(coeff_kernel, A, R, H), out_shape=jax.Sh...  87.7 us
    pallas_call x1, Pallas kernels, update(): pl.pallas_call(functools.partial(update_kernel, M, X, NC, CW, RB, 256), o...  80.4 us
    unnamed x9, local copies, waits for them, and re-layouts  8.03 us

profile of v1, /device:TPU:0, one launch (start us, length us, event | category | flops | bytes accessed | tf_op | source)
XLA Modules:
  0.0 179.3 jit_solution(5755665466869140711)
XLA Ops:
  0.0 0.8 fusion
  0.8 0.7 reduce
  1.6 0.7 copy.16
  2.3 1.2 copy.17
  3.5 0.3 copy.15
  3.8 0.0 copy-start.1
  3.8 1.6 copy-done.1
  5.4 87.7 %shard_map.64.coef = bf16[1536,512]{1,0:T(8,128)(2,1)S(1)} custom-call(bf16[1536,2048]{1,0:T(8,128)(2,1)} %bitcast.13, bf16[16,2048]{1,0:T(8,128)(2,1)S(1)} %broadcast_in_dim.9.pha, f32[1536,1]{1,0:T(8,128)S(1)} %bitcast.11, bf16[2048,512]{1,0:T(8,128)(2,1)S(1)} %copy-done.1), custom_call_target="tpu_custom_call" | custom-call | tf_op jit(solution)/shard_map/pallas_call | solution.py:200
  93.1 0.0 copy-start
  93.1 1.1 copy-done
  94.2 1.6 copy.12
  95.8 80.4 %shard_map.65 = f32[128,4096]{1,0:T(8,128)} custom-call(bf16[1536,512]{1,0:T(8,128)(2,1)} %copy-done, bf16[512,1536]{1,0:T(8,128)(2,1)} %bitcast.12, s32[1536,1]{1,0:T(8,128)} %bitcast.14, bf16[512,4096]{1,0:T(8,128)(2,1)} %refs.1), custom_call_target="tpu_custom_call" | custom-call | tf_op jit(solution)/shard_map/pallas_call | solution.py:380
  176.2 3.1 %copy.19 = f32[128,4096]{1,0:T(8,128)} copy(f32[128,4096]{1,0:T(8,128)} %shard_map.65) | data formatting | bytes 4194304
  (3 shorter events, 0.0 us)
Async XLA Ops:
  3.8 1.6 copy-start.1
  93.1 1.1 copy-start
